TPU v7x, 32 devices: a whole 2x2x4 slice. The times are simulated.
32 devices in a mesh: fsdp: 4 (over x, core), ep: 8 (over z, y).
Axes of the slice: x: 2, y: 2, z: 4, core: 2. Of those that a mesh axis runs over, the one named last changes fastest.
Arguments:
- tokens: bfloat16 [256, 2048], P(('fsdp', 'ep')), may hold values from -6 to 6
- cotangent: bfloat16 [256, 2048], P(('fsdp', 'ep')), may hold values from -4 to 4
- routes: int32 [256, 2], P(('fsdp', 'ep')), may hold values from 0 to 7, as said below
- logits: float32 [256, 8], P(('fsdp', 'ep')), may hold values from -8 to 8
- w_gate: bfloat16 [2048, 16384], P('fsdp', 'ep'), may hold values from -0.125 to 0.125
- w_up: bfloat16 [2048, 16384], P('fsdp', 'ep'), may hold values from -0.125 to 0.125
- w_down: bfloat16 [16384, 2048], P('ep', 'fsdp'), may hold values from -0.0625 to 0.0625
Outputs:
- grad_tokens: bfloat16 [256, 2048], P(('fsdp', 'ep'))
- route_dot: float32 [256, 2], P(('fsdp', 'ep'))
- aux_grad: float32 [256, 8], P(('fsdp', 'ep'))
- grad_gate: bfloat16 [2048, 16384], P('fsdp', 'ep')
- grad_up: bfloat16 [2048, 16384], P('fsdp', 'ep')
- grad_down: bfloat16 [16384, 2048], P('ep', 'fsdp')
Inputs may be any that keep to these rules, and one draw needn't show every extreme that they name: `routes`: each token names two different experts; on every device at most 3 tokens name one expert, and some expert is named by exactly 3 of them.
All inputs are finite; a program needn't handle non-finite values.
Results may differ from a plain program's by a relative error of at most 0.04.
Values may be sent and summed in bfloat16 or wider, within the bound.
A program may use at most 128 MiB of HBM per device.

v0:
```python
import jax
import jax.numpy as jnp
from jax import lax
from jax.sharding import PartitionSpec as P

EXP_WIN = 2
CAP = 3


def routing(routes, logits):
    experts_all = logits.shape[-1]
    picked = (routes[:, :, None] == jnp.arange(experts_all, dtype=jnp.int32)[None, None, :]).astype(
        jnp.float32
    )
    chosen = jnp.sum(picked * logits[:, None, :], axis=2)
    combine = jax.nn.softmax(chosen, axis=1)
    window = picked[:, :, :EXP_WIN]
    member = jnp.sum(window, axis=1)
    scaled = jnp.sum(window * combine[:, :, None], axis=1)
    member_int = member.astype(jnp.int32)
    slot_ids = jnp.cumsum(member_int, axis=0) - member_int
    places = jnp.arange(CAP, dtype=jnp.int32)
    select = member[:, :, None] * (slot_ids[:, :, None] == places[None, None, :]).astype(
        jnp.float32
    )
    select = jnp.transpose(select, (1, 2, 0))
    slot_weight = jnp.einsum("xct,tx->xc", select, scaled)
    return (select, slot_weight)


def dispatch(select, slot_weight, tokens, cotangent):
    sent_tokens = jnp.einsum("xct,td->xcd", select, tokens.astype(jnp.float32)).astype(jnp.bfloat16)
    moved = jnp.einsum("xct,td->xcd", select, cotangent.astype(jnp.float32))
    sent_grads = (moved * slot_weight[:, :, None]).astype(jnp.bfloat16)
    return (sent_tokens, sent_grads)


def aux_gradient(logits, total_counts):
    frac = total_counts.astype(jnp.float32) / jnp.sum(total_counts.astype(jnp.float32))
    probs = jax.nn.softmax(logits, axis=1)
    target = logits.shape[1] * frac
    return probs * (target[None, :] - jnp.sum(probs * target[None, :], axis=1, keepdims=True))


def body(tokens, cotangent, routes, logits, w_gate, w_up, w_down):
    n_peers = lax.axis_size("ep")
    blocks = n_peers // EXP_WIN
    width_model = tokens.shape[1]
    width_local = w_gate.shape[1]
    experts_all = logits.shape[1]
    local_counts = jnp.sum(
        (routes[:, :, None] == jnp.arange(experts_all, dtype=jnp.int32)[None, None, :]).astype(
            jnp.int32
        ),
        axis=(0, 1),
    )
    total_counts = lax.psum(local_counts, ("fsdp", "ep"))
    aux_grad = aux_gradient(logits, total_counts)
    select, slot_weight = routing(routes, logits)
    sent_tokens, sent_grads = dispatch(select, slot_weight, tokens, cotangent)
    send_tokens = jnp.repeat(sent_tokens, blocks, axis=0)
    send_grads = jnp.repeat(sent_grads, blocks, axis=0)
    came_tokens, came_grads = (
        lax.all_to_all(send_tokens, "ep", split_axis=0, concat_axis=0, tiled=True),
        lax.all_to_all(send_grads, "ep", split_axis=0, concat_axis=0, tiled=True),
    )
    nrows = came_tokens.shape[0] * came_tokens.shape[1]
    rows_x = came_tokens.reshape(nrows, width_model)
    rows_dy = came_grads.reshape(nrows, width_model)
    gate_full, up_full, down_full = (
        lax.all_gather(w_gate, "fsdp", axis=0, tiled=True),
        lax.all_gather(w_up, "fsdp", axis=0, tiled=True),
        lax.all_gather(w_down, "fsdp", axis=1, tiled=True),
    )
    gate_pre = jnp.dot(rows_x, gate_full, preferred_element_type=jnp.float32)
    up_pre = jnp.dot(rows_x, up_full, preferred_element_type=jnp.float32)
    hidden_grad = lax.dot_general(
        rows_dy, down_full, (((1,), (1,)), ((), ())), preferred_element_type=jnp.float32
    )
    sigma = jax.nn.sigmoid(gate_pre)
    active = gate_pre * sigma
    hidden = (active * up_pre).astype(jnp.bfloat16)
    part_dot = jnp.sum(hidden.astype(jnp.float32) * hidden_grad, axis=1).astype(jnp.bfloat16)
    up_grad = (hidden_grad * active).astype(jnp.bfloat16)
    gate_grad = (hidden_grad * up_pre * sigma * (1.0 + gate_pre * (1.0 - sigma))).astype(
        jnp.bfloat16
    )
    contract_last = (((1,), (1,)), ((), ()))
    part_x = lax.dot_general(
        gate_grad, gate_full, contract_last, preferred_element_type=jnp.float32
    )
    part_x = (
        part_x
        + lax.dot_general(up_grad, up_full, contract_last, preferred_element_type=jnp.float32)
    ).astype(jnp.bfloat16)
    back_x, back_dot = (
        lax.all_to_all(
            part_x.reshape(n_peers, CAP, width_model), "ep", split_axis=0, concat_axis=0, tiled=True
        ),
        lax.all_to_all(
            part_dot.reshape(n_peers, CAP), "ep", split_axis=0, concat_axis=0, tiled=True
        ),
    )
    slot_grad = jnp.sum(
        back_x.astype(jnp.float32).reshape(EXP_WIN, blocks, CAP, width_model), axis=1
    )
    slot_dot = jnp.sum(back_dot.astype(jnp.float32).reshape(EXP_WIN, blocks, CAP), axis=1)
    grad_tokens = jnp.einsum("xct,xcd->td", select, slot_grad).astype(jnp.bfloat16)
    route_dot = jnp.einsum("xct,xc->tx", select, slot_dot)
    contract_first = (((0,), (0,)), ((), ()))
    summed = lax.psum_scatter(
        jnp.concatenate(
            [
                lax.dot_general(
                    rows_x, gate_grad, contract_first, preferred_element_type=jnp.float32
                ),
                lax.dot_general(
                    rows_x, up_grad, contract_first, preferred_element_type=jnp.float32
                ),
                lax.dot_general(
                    rows_dy, hidden, contract_first, preferred_element_type=jnp.float32
                ),
            ],
            axis=1,
        ).astype(jnp.bfloat16),
        "fsdp",
        scatter_dimension=0,
        tiled=True,
    ).astype(jnp.float32)
    grad_gate = summed[:, :width_local].astype(jnp.bfloat16)
    grad_up = summed[:, width_local : 2 * width_local].astype(jnp.bfloat16)
    grad_down = jnp.transpose(summed[:, 2 * width_local :]).astype(jnp.bfloat16)
    return (grad_tokens, route_dot, aux_grad, grad_gate, grad_up, grad_down)


def solution(mesh):
    in_specs = (
        P(("fsdp", "ep"), None),
        P(("fsdp", "ep"), None),
        P(("fsdp", "ep"), None),
        P(("fsdp", "ep"), None),
        P("fsdp", "ep"),
        P("fsdp", "ep"),
        P("ep", "fsdp"),
    )
    out_specs = (
        P(("fsdp", "ep"), None),
        P(("fsdp", "ep"), None),
        P(("fsdp", "ep"), None),
        P("fsdp", "ep"),
        P("fsdp", "ep"),
        P("ep", "fsdp"),
    )
    return jax.shard_map(body, mesh=mesh, in_specs=in_specs, out_specs=out_specs, check_vma=False)
```

profile of v0, /device:TPU:0, one launch (start us, length us, event | category | flops | bytes accessed | tf_op | source)
XLA Modules:
  0.0 424.8 jit_solution(4245752943152439672)
XLA Ops:
  12.3 7.3 %all-to-all-start.1 = ((bf16[8,3,2048]{2,1,0:T(4,128)(2,1)}), bf16[8,3,2048]{2,1,0:T(4,128)(2,1)S(1)}, u32[]{:S(2)}, u32[]{:S(2)}) async-start(bf16[8,3,2048]{2,1,0:T(4,128)(2,1)} %bitcast.9), calls=%async_computation.1 | async-start | bytes 262144 | tf_op jit(solution)/shard_map/all_to_all | solution.py:64
  20.7 6.2 %all-to-all-done.1 = bf16[8,3,2048]{2,1,0:T(4,128)(2,1)S(1)} async-done(((bf16[8,3,2048]{2,1,0:T(4,128)(2,1)}), bf16[8,3,2048]{2,1,0:T(4,128)(2,1)S(1)}, u32[]{:S(2)}, u32[]{:S(2)}) %all-to-all-start.1) | async-done | bytes 98336 | tf_op jit(solution)/shard_map/all_to_all | solution.py:64
  27.6 3.4 all-to-all-start
  31.1 7.1 %all-to-all-done = bf16[8,3,2048]{2,1,0:T(4,128)(2,1)S(1)} async-done(((bf16[8,3,2048]{2,1,0:T(4,128)(2,1)}), bf16[8,3,2048]{2,1,0:T(4,128)(2,1)S(1)}, u32[]{:S(2)}, u32[]{:S(2)}) %all-to-all-start) | async-done | bytes 98336 | tf_op jit(solution)/shard_map/all_to_all | solution.py:65
  38.4 32.2 %all-gather.8.cloned.1.call-done = bf16[2048,2048]{1,0:T(8,128)(2,1)} async-done(((bf16[512,2048]{1,0:T(8,128)(2,1)}), bf16[2048,2048]{1,0:T(8,128)(2,1)}) %all-gather.8.cloned.1.call-update) | async-done | bytes 8388624 | tf_op jit(solution)/shard_map/all_gather | solution.py:71
  70.6 4.6 %fusion.38 = f32[24,2048]{1,0:T(8,128)S(1)} fusion(bf16[24,2048]{1,0:T(8,128)(2,1)S(1)} %reshape.110, bf16[2048,2048]{1,0:T(8,128)(2,1)} %all-gather.8.cloned.1.call-done), kind=kOutput, calls=%fused_computation.67 | convolution fusion | flops 201326592 | bytes 8683520 | tf_op jit(solution)/shard_map/dot_general | solution.py:75
  75.1 55.3 %all-gather.6.cloned.1.call-done = bf16[2048,2048]{1,0:T(8,128)(2,1)} async-done(((bf16[512,2048]{1,0:T(8,128)(2,1)}), bf16[2048,2048]{1,0:T(8,128)(2,1)}) %all-gather.6.cloned.1.call-update) | async-done | bytes 8388624 | tf_op jit(solution)/shard_map/all_gather | solution.py:72
  130.4 4.6 %fusion.37 = f32[24,2048]{1,0:T(8,128)S(1)} fusion(bf16[24,2048]{1,0:T(8,128)(2,1)S(1)} %reshape.110, bf16[2048,2048]{1,0:T(8,128)(2,1)} %all-gather.6.cloned.1.call-done), kind=kOutput, calls=%fused_computation.66 | convolution fusion | flops 201326592 | bytes 8683520 | tf_op jit(solution)/shard_map/dot_general | solution.py:76
  135.0 55.3 %all-gather.4.cloned.1.call-done = bf16[2048,2048]{1,0:T(8,128)(2,1)} async-done(((bf16[2048,512]{1,0:T(8,128)(2,1)}), bf16[2048,2048]{1,0:T(8,128)(2,1)}) %all-gather.4.cloned.1.call-update) | async-done | bytes 8388624 | tf_op jit(solution)/shard_map/all_gather | solution.py:73
  190.3 5.8 %multiply_reduce_fusion = (bf16[24]{0:T(256)(128)(2,1)S(1)}, bf16[24,2048]{1,0:T(8,128)(2,1)S(1)}, bf16[24,2048]{1,0:T(8,128)(2,1)S(1)}, bf16[24,2048]{1,0:T(8,128)(2,1)S(1)}) fusion(f32[24,2048]{1,0:T(8,128)S(1)} %fusion.37, f32[24,2048]{1,0:T(8,128)S(1)} %fusion.38, bf16[24,2048]{1,0:T(8,128)(2,1)S(1)} %reshape.108, ...), kind=kOutput, calls=%fused_computation.13 | convolution fusion | flops 202211296 | bytes 9175088 | tf_op jit(solution)/shard_map/dot_general | solution.py:77
  196.1 5.6 %convolution_convert_fusion = bf16[2048,2048]{0,1:T(8,128)(2,1)} fusion(bf16[24,2048]{1,0:T(8,128)(2,1)S(1)} %reshape.108, bf16[24,2048]{1,0:T(8,128)(2,1)S(1)} %get-tuple-element.39), kind=kOutput, calls=%fused_computation.1 | convolution fusion | flops 205520896 | bytes 8585216 | tf_op jit(solution)/shard_map/dot_general | solution.py:120
  201.7 5.6 %convolution_convert_fusion.2 = bf16[2048,2048]{0,1:T(8,128)(2,1)} fusion(bf16[24,2048]{1,0:T(8,128)(2,1)S(1)} %reshape.110, bf16[24,2048]{1,0:T(8,128)(2,1)S(1)} %get-tuple-element.43), kind=kOutput, calls=%fused_computation.3 | convolution fusion | flops 205520896 | bytes 8585216 | tf_op jit(solution)/shard_map/dot_general | solution.py:114
  207.2 5.6 %convolution_convert_fusion.1 = bf16[2048,2048]{0,1:T(8,128)(2,1)} fusion(bf16[24,2048]{1,0:T(8,128)(2,1)S(1)} %reshape.110, bf16[24,2048]{1,0:T(8,128)(2,1)S(1)} %get-tuple-element.44), kind=kOutput, calls=%fused_computation.2 | convolution fusion | flops 205520896 | bytes 8585216 | tf_op jit(solution)/shard_map/dot_general | solution.py:117
  212.8 18.0 %pad_maximum_fusion = bf16[2048,6144]{0,1:T(8,128)(2,1)} fusion(bf16[2048,2048]{0,1:T(8,128)(2,1)} %convolution_convert_fusion, bf16[2048,2048]{0,1:T(8,128)(2,1)} %convolution_convert_fusion.1, bf16[2048,2048]{0,1:T(8,128)(2,1)} %convolution_convert_fusion.2), kind=kLoop, calls=%fused_computation | loop fusion | flops 75497472 | bytes 50331648 | tf_op jit(solution)/shard_map/concatenate | solution.py:112
  231.5 39.6 %psum.7 = s32[8]{0:T(128)S(1)} all-reduce(s32[8]{0:T(128)S(1)} %convert_reduce_fusion.1), channel_id=1, replica_groups=mesh['fsdp'=4,'ep'=8] {'fsdp','ep'}, use_global_device_ids=true, to_apply=%region_12.13 | all-reduce | flops 8 | bytes 64 | tf_op jit(solution)/shard_map/psum | solution.py:57
  274.3 5.2 %all-to-all-start.3 = ((bf16[8,1,3]{2,1,0:T(2,128)(2,1)}), bf16[8,1,3]{2,1,0:T(2,128)(2,1)S(1)}, u32[]{:S(2)}, u32[]{:S(2)}) async-start(bf16[8,1,3]{2,1,0:T(2,128)(2,1)} %convert_element_type.101), calls=%async_computation.3 | async-start | bytes 8192 | tf_op jit(solution)/shard_map/all_to_all | solution.py:100
  279.5 6.1 %fusion.39 = f32[24,2048]{1,0:T(8,128)S(1)} fusion(bf16[24,2048]{1,0:T(8,128)(2,1)S(1)} %get-tuple-element.43, bf16[2048,2048]{1,0:T(8,128)(2,1)} %all-gather.8.cloned.1.call-done), kind=kOutput, calls=%fused_computation.68 | convolution fusion | flops 201326592 | bytes 8683520 | tf_op jit(solution)/shard_map/dot_general | solution.py:89
  285.5 5.7 %fusion = bf16[24,2048]{1,0:T(8,128)(2,1)S(1)} fusion(f32[24,2048]{1,0:T(8,128)S(1)} %fusion.39, bf16[24,2048]{1,0:T(8,128)(2,1)S(1)} %get-tuple-element.44, bf16[2048,2048]{1,0:T(8,128)(2,1)} %all-gather.6.cloned.1.call-done), kind=kOutput, calls=%fused_computation.5 | convolution fusion | flops 201424896 | bytes 8781824 | tf_op jit(solution)/shard_map/dot_general | solution.py:94
  291.9 6.0 %all-to-all-start.2 = ((bf16[8,3,2048]{2,1,0:T(4,128)(2,1)}), bf16[8,3,2048]{2,1,0:T(4,128)(2,1)S(1)}, u32[]{:S(2)}, u32[]{:S(2)}) async-start(bf16[8,3,2048]{2,1,0:T(4,128)(2,1)} %reshape.111), calls=%async_computation.2 | async-start | bytes 262144 | tf_op jit(solution)/shard_map/all_to_all | solution.py:97
  299.0 6.2 %all-to-all-done.2 = bf16[8,3,2048]{2,1,0:T(4,128)(2,1)S(1)} async-done(((bf16[8,3,2048]{2,1,0:T(4,128)(2,1)}), bf16[8,3,2048]{2,1,0:T(4,128)(2,1)S(1)}, u32[]{:S(2)}, u32[]{:S(2)}) %all-to-all-start.2) | async-done | bytes 98336 | tf_op jit(solution)/shard_map/all_to_all | solution.py:97
  306.2 100.5 %reduce-scatter.2.cloned.1.call-done = bf16[512,6144]{0,1:T(8,128)(2,1)} async-done(((bf16[2048,6144]{0,1:T(8,128)(2,1)}), bf16[512,6144]{0,1:T(8,128)(2,1)}) %reduce-scatter.2.cloned.1.call-update) | async-done | bytes 6291472 | tf_op jit(solution)/shard_map/reduce_scatter | solution.py:111
  406.7 5.3 %slice_bitcast_fusion = (bf16[2048,512]{1,0:T(8,128)(2,1)}, bf16[512,2048]{0,1:T(8,128)(2,1)}, bf16[512,2048]{0,1:T(8,128)(2,1)S(1)}) fusion(bf16[512,6144]{0,1:T(8,128)(2,1)} %reduce-scatter.2.cloned.1.call-done), kind=kLoop, calls=%fused_computation.11 | loop fusion | bytes 12582912 | tf_op jit(solution)/shard_map/convert_element_type | solution.py:132
  412.0 3.9 copy.37
  415.9 2.4 copy.36
  (52 shorter events, 13.6 us)
Async XLA Ops:
  7.2 4.3 %copy-start = (bf16[8,2048]{1,0:T(8,128)(2,1)S(1)}, bf16[8,2048]{1,0:T(8,128)(2,1)}, u32[]{:S(2)}) copy-start(bf16[8,2048]{1,0:T(8,128)(2,1)} %param.7) | copy-start | bytes 98308
  7.2 63.4 %all-gather.8.cloned.1.call-start = ((), (), s32[]{:S(2)}) async-start(), calls=%async_computation.7 | async-start | bytes 10485760 | tf_op jit(solution)/shard_map/all_gather | solution.py:71
  7.9 122.5 %all-gather.6.cloned.1.call-start = ((), (), s32[]{:S(2)}) async-start(), calls=%async_computation.6 | async-start | bytes 10485760 | tf_op jit(solution)/shard_map/all_gather | solution.py:72
  8.7 181.6 %all-gather.4.cloned.1.call-start = ((), (), s32[]{:S(2)}) async-start(), calls=%async_computation.5 | async-start | bytes 10485760 | tf_op jit(solution)/shard_map/all_gather | solution.py:73
  12.3 14.7 %all-to-all-start.1 = ((bf16[8,3,2048]{2,1,0:T(4,128)(2,1)}), bf16[8,3,2048]{2,1,0:T(4,128)(2,1)S(1)}, u32[]{:S(2)}, u32[]{:S(2)}) async-start(bf16[8,3,2048]{2,1,0:T(4,128)(2,1)} %bitcast.9), calls=%async_computation.1 | async-start | bytes 262144 | tf_op jit(solution)/shard_map/all_to_all | solution.py:64
  27.6 10.7 %all-to-all-start = ((bf16[8,3,2048]{2,1,0:T(4,128)(2,1)}), bf16[8,3,2048]{2,1,0:T(4,128)(2,1)S(1)}, u32[]{:S(2)}, u32[]{:S(2)}) async-start(bf16[8,3,2048]{2,1,0:T(4,128)(2,1)} %bitcast.7), calls=%async_computation | async-start | bytes 262144 | tf_op jit(solution)/shard_map/all_to_all | solution.py:65
  31.0 375.7 %reduce-scatter.2.cloned.1.call-start = ((), (), s32[]{:S(2)}) async-start(), calls=%async_computation.8 | async-start | bytes 31457280 | tf_op jit(solution)/shard_map/reduce_scatter | solution.py:111
  230.8 0.7 copy-start.3
  230.8 40.4 %copy-start.2 = (f32[8,8]{1,0:T(8,128)S(1)}, f32[8,8]{1,0:T(8,128)}, u32[]{:S(2)}) copy-start(f32[8,8]{1,0:T(8,128)} %param.10) | copy-start | bytes 772
  274.3 17.7 %all-to-all-start.3 = ((bf16[8,1,3]{2,1,0:T(2,128)(2,1)}), bf16[8,1,3]{2,1,0:T(2,128)(2,1)S(1)}, u32[]{:S(2)}, u32[]{:S(2)}) async-start(bf16[8,1,3]{2,1,0:T(2,128)(2,1)} %convert_element_type.101), calls=%async_computation.3 | async-start | bytes 8192 | tf_op jit(solution)/shard_map/all_to_all | solution.py:100
  291.9 13.3 %all-to-all-start.2 = ((bf16[8,3,2048]{2,1,0:T(4,128)(2,1)}), bf16[8,3,2048]{2,1,0:T(4,128)(2,1)S(1)}, u32[]{:S(2)}, u32[]{:S(2)}) async-start(bf16[8,3,2048]{2,1,0:T(4,128)(2,1)} %reshape.111), calls=%async_computation.2 | async-start | bytes 262144 | tf_op jit(solution)/shard_map/all_to_all | solution.py:97
  305.4 112.9 %copy-start.1 = (bf16[8,2048]{1,0:T(8,128)(2,1)S(1)}, bf16[8,2048]{1,0:T(8,128)(2,1)}, u32[]{:S(2)}) copy-start(bf16[8,2048]{1,0:T(8,128)(2,1)} %param.7) | copy-start | bytes 98308
Sparse Core Ops, SparseCore 0:
  9.5 60.9 all-gather.7
  72.1 58.2 all-gather.5
  132.0 58.2 all-gather.3
  230.9 175.7 reduce-scatter.1
where the time goes:
time: 426 us; the launch traced here: 425 us
  waiting for transfers between devices  265 us (62%)
  matrix products  46.1 us (11%)
  blocking collectives  39.6 us (9%)
  other arithmetic  22.6 us (5%)
  starting transfers between devices  22 us (5%)
  local copies, waits for them, and re-layouts  15.6 us (4%)
  between operations  13.9 us (3%)
    reduce_scatter x1, waiting for transfers between devices, body(): lax.psum_scatter(jnp.concatenate([lax.dot_general(rows_x, gate_grad, cont...  101 us
    all_gather x1, waiting for transfers between devices, body(): lax.all_gather(w_down, 'fsdp', axis=1, tiled=True)  55.3 us
    all_gather x1, waiting for transfers between devices, body(): lax.all_gather(w_up, 'fsdp', axis=0, tiled=True)  55.3 us
    psum x1, blocking collectives, body(): total_counts = lax.psum(local_counts, ('fsdp', 'ep'))  39.6 us
    all_gather x1, waiting for transfers between devices, body(): lax.all_gather(w_gate, 'fsdp', axis=0, tiled=True)  32.2 us
    concatenate x1, other arithmetic, body(): jnp.concatenate([lax.dot_general(rows_x, gate_grad, contract_first, prefe...  18 us
  transfers between devices with their start and end apart: 8, of which 7 were waited for; matrix products, arithmetic and copies ran while one was open for 7% of the time, Pallas kernels for 0%

commit v1 on v0

v1 whole, which is shorter than its diff:
```python
import functools

import jax
import jax.numpy as jnp
from jax import lax
from jax.experimental import pallas as pl
from jax.experimental.pallas import tpu as pltpu
from jax.sharding import PartitionSpec as P

EXP_WIN = 2
CAP = 3
PAD = 8
CORES = 2
CHUNKS = 4
LAST = (((1,), (1,)), ((), ()))
FIRST = (((0,), (0,)), ((), ()))
F32 = jnp.float32
BF16 = jnp.bfloat16
MESH = pl.DeviceIdType.MESH


def iota(shape, axis):
    return lax.broadcasted_iota(jnp.int32, shape, axis)


def kernel(
    n_fsdp, n_ep, chunks,
    tok_ref, cot_ref, routes_ref, logits_ref, wg_hbm, wu_hbm, wd_hbm,
    gt_ref, rd_ref, aux_ref, gg_hbm, gu_hbm, gd_hbm,
    wg, wu, wd, og, ou, od,
    send1, recv1, rows_x, rows_dy,
    own_a, send_a, recv_a, send_b, recv_b, acts, recv_c, dx, dots, send2, recv2,
    w_sem, o_sem, d_send, d_recv, a_send, a_recv, b_send, b_recv, c_send, c_recv, r_send, r_recv,
):
    n_dev = n_fsdp * n_ep
    n_x = n_fsdp // CORES
    blocks = n_ep // EXP_WIN
    f, e = lax.axis_index("fsdp"), lax.axis_index("ep")
    me = f * n_ep + e
    x, core = f // CORES, lax.rem(f, CORES)
    partner = x * CORES + (1 - core)
    depth, width = wg.shape
    half = width // CORES
    w = half // chunks

    barrier = pltpu.get_barrier_semaphore()

    def greet(j, _):
        d = lax.rem(me + j, n_dev)
        pl.semaphore_signal(barrier, inc=1, device_id=(d // n_ep, lax.rem(d, n_ep)), device_id_type=MESH)
        return 0

    lax.fori_loop(1, n_dev, greet, 0)
    loads = [
        pltpu.make_async_copy(s, t, w_sem.at[i])
        for i, (s, t) in enumerate(((wg_hbm, wg), (wu_hbm, wu), (wd_hbm, wd)))
    ]
    for c in loads:
        c.start()

    routes = routes_ref[...]
    logits = logits_ref[...]
    n_tok, n_exp = logits.shape
    r0, r1 = routes[:, 0:1], routes[:, 1:2]
    experts = iota((n_tok, n_exp), 1)
    c0 = jnp.sum(jnp.where(experts == r0, logits, 0.0), axis=1, keepdims=True)
    c1 = jnp.sum(jnp.where(experts == r1, logits, 0.0), axis=1, keepdims=True)
    top = jnp.maximum(c0, c1)
    e0, e1 = jnp.exp(c0 - top), jnp.exp(c1 - top)
    p0, p1 = e0 / (e0 + e1), e1 / (e0 + e1)
    ti, tj = iota((n_tok, n_tok), 0), iota((n_tok, n_tok), 1)
    ci = iota((PAD, n_tok), 0)
    lanes = iota((n_tok, depth), 1)
    counts = jnp.sum(
        jnp.where(lanes == r0, 1.0, 0.0) + jnp.where(lanes == r1, 1.0, 0.0), axis=0, keepdims=True
    )
    tok = tok_ref[...]
    cot = cot_ref[...].astype(F32)
    member_col, slot_col = [], []
    row_id = iota((PAD, depth), 0)
    for k in range(EXP_WIN):
        m0, m1 = jnp.where(r0 == k, 1.0, 0.0), jnp.where(r1 == k, 1.0, 0.0)
        col = m0 + m1
        weight = m0 * p0 + m1 * p1
        row = jnp.sum(jnp.where(ti == tj, col, 0.0), axis=0, keepdims=True)
        slot_row = jnp.sum(jnp.where(ti < tj, col, 0.0), axis=0, keepdims=True)
        slot_col.append(jnp.sum(jnp.where(tj < ti, row, 0.0), axis=1, keepdims=True))
        member_col.append(col)
        cf = ci.astype(F32)
        sel_a = jnp.where((cf == slot_row) & (ci < CAP), row, 0.0).astype(BF16)
        sel_b = jnp.where((cf - CAP == slot_row) & (ci < 2 * CAP), row, 0.0).astype(BF16)
        wcot = (cot * weight).astype(BF16)
        sent = jnp.dot(sel_a, tok, preferred_element_type=F32)
        sent = sent + jnp.dot(sel_b, wcot, preferred_element_type=F32)
        for g in range(n_fsdp):
            part = sent[:, g * depth : (g + 1) * depth]
            send1[k, g] = jnp.where(row_id == 2 * CAP, counts, part).astype(BF16)

    pl.semaphore_wait(barrier, n_dev - 1)

    def push(j, _):
        d = lax.rem(me + j, n_dev)
        df, de = d // n_ep, lax.rem(d, n_ep)
        pltpu.make_async_remote_copy(
            src_ref=send1.at[de // blocks, df], dst_ref=recv1.at[me], send_sem=d_send, recv_sem=d_recv,
            device_id=(df, de), device_id_type=MESH,
        ).start()
        return 0

    lax.fori_loop(1, n_dev, push, 0)
    recv1[me] = send1[e // blocks, f]
    everyone = recv1.at[pl.ds(0, n_dev - 1)]
    pltpu.make_async_copy(everyone, everyone, d_recv).wait()

    grp = min(32, n_dev)
    si, sj = iota((grp * CAP, grp * PAD), 0), iota((grp * CAP, grp * PAD), 1)
    base = (si // CAP) * PAD + lax.rem(si, CAP)
    pick_x = jnp.where(sj == base, 1.0, 0.0).astype(BF16)
    pick_dy = jnp.where(sj == base + CAP, 1.0, 0.0).astype(BF16)
    pick_c = jnp.where(
        lax.rem(iota((8, grp * PAD), 1), PAD) == 2 * CAP, 1.0, 0.0
    ).astype(BF16)
    total = jnp.zeros((8, depth), F32)
    for g in range(n_dev // grp):
        came = recv1[g * grp : (g + 1) * grp].reshape(grp * PAD, depth)
        span = pl.ds(g * grp * CAP, grp * CAP)
        rows_x[span] = jnp.dot(pick_x, came, preferred_element_type=F32).astype(BF16)
        rows_dy[span] = jnp.dot(pick_dy, came, preferred_element_type=F32).astype(BF16)
        total = total + jnp.dot(pick_c, came, preferred_element_type=F32)

    def copy_a(k):
        return pltpu.make_async_remote_copy(
            src_ref=send_a.at[k], dst_ref=recv_a.at[k], send_sem=a_send.at[k], recv_sem=a_recv.at[k],
            device_id=(partner, e), device_id_type=MESH,
        )

    def copy_b(k, j):
        to = lax.rem(x + j, n_x) * CORES + core
        return pltpu.make_async_remote_copy(
            src_ref=send_b.at[k], dst_ref=recv_b.at[k, j - 1], send_sem=b_send.at[k, j - 1],
            recv_sem=b_recv.at[k, j - 1], device_id=(to, e), device_id_type=MESH,
        )

    def copy_c(k):
        return pltpu.make_async_remote_copy(
            src_ref=acts.at[k], dst_ref=recv_c.at[k], send_sem=c_send.at[k], recv_sem=c_recv.at[k],
            device_id=(partner, e), device_id_type=MESH,
        )

    def columns(h, k):
        return pl.ds(pl.multiple_of(h * half + k * w, w), w)

    def partials(h, k):
        cols = columns(h, k)
        xs, dys = rows_x[...], rows_dy[...]
        yield jnp.dot(xs, wg[:, cols], preferred_element_type=F32)
        yield jnp.dot(xs, wu[:, cols], preferred_element_type=F32)
        yield lax.dot_general(dys, wd[cols, :], LAST, preferred_element_type=F32)

    def stage1(k):
        for i, v in enumerate(partials(1 - core, k)):
            send_a[k, i] = v.astype(BF16)
        copy_a(k).start()
        for i, v in enumerate(partials(core, k)):
            own_a[k, i] = v

    def stage2(k):
        copy_a(k).wait_recv()
        v = own_a[k] + recv_a[k].astype(F32)
        own_a[k] = v
        send_b[k] = v.astype(BF16)
        for j in range(1, n_x):
            copy_b(k, j).start()

    def stage3(k):
        for j in range(1, n_x):
            copy_b(k, j).wait_recv()
        pre = []
        for i in range(3):
            v = own_a[k, i]
            for j in range(n_x - 1):
                v = v + recv_b[k, j, i].astype(F32)
            pre.append(v)
        gate_pre, up_pre, hidden_grad = pre
        sigma = jax.nn.sigmoid(gate_pre)
        active = gate_pre * sigma
        hidden = (active * up_pre).astype(BF16)
        dot = jnp.sum(hidden.astype(F32) * hidden_grad, axis=1, keepdims=True)
        dots[...] = dot if k == 0 else dots[...] + dot
        acts[k, 0] = (hidden_grad * up_pre * sigma * (1.0 + gate_pre * (1.0 - sigma))).astype(BF16)
        acts[k, 1] = (hidden_grad * active).astype(BF16)
        acts[k, 2] = hidden
        copy_c(k).start()

    outs = ((og, gg_hbm), (ou, gu_hbm))

    def grads(h, k, source):
        cols = columns(h, k)
        xs, dys = rows_x[...], rows_dy[...]
        gate_grad, up_grad, hidden = source[k, 0], source[k, 1], source[k, 2]
        part = lax.dot_general(gate_grad, wg[:, cols], LAST, preferred_element_type=F32)
        part = part + lax.dot_general(up_grad, wu[:, cols], LAST, preferred_element_type=F32)
        og[:, cols] = lax.dot_general(xs, gate_grad, FIRST, preferred_element_type=F32).astype(BF16)
        ou[:, cols] = lax.dot_general(xs, up_grad, FIRST, preferred_element_type=F32).astype(BF16)
        od[cols, :] = lax.dot_general(hidden, dys, FIRST, preferred_element_type=F32).astype(BF16)
        return part

    def stores(h, k, slot):
        cols = columns(h, k)
        return [
            pltpu.make_async_copy(og.at[:, cols], gg_hbm.at[:, cols], o_sem.at[k, slot, 0]),
            pltpu.make_async_copy(ou.at[:, cols], gu_hbm.at[:, cols], o_sem.at[k, slot, 1]),
            pltpu.make_async_copy(od.at[cols, :], gd_hbm.at[cols, :], o_sem.at[k, slot, 2]),
        ]

    def stage4(k):
        part = grads(core, k, acts)
        for c in stores(core, k, 0):
            c.start()
        copy_c(k).wait_recv()
        part = part + grads(1 - core, k, recv_c)
        for c in stores(1 - core, k, 1):
            c.start()
        dx[...] = part if k == 0 else dx[...] + part

    for c in loads:
        c.wait()
    stage1(0)
    for k in range(1, chunks):
        stage1(k)
        stage2(k - 1)
    stage2(chunks - 1)

    count = total[0:1, 0:n_exp]
    target = n_exp * (count / jnp.sum(count, axis=1, keepdims=True))
    raised = jnp.exp(logits - jnp.max(logits, axis=1, keepdims=True))
    probs = raised / jnp.sum(raised, axis=1, keepdims=True)
    aux_ref[...] = probs * (target - jnp.sum(probs * target, axis=1, keepdims=True))

    stage3(0)
    for k in range(1, chunks):
        stage3(k)
        stage4(k - 1)
    stage4(chunks - 1)

    bi, bj = iota((grp * PAD, grp * CAP), 0), iota((grp * PAD, grp * CAP), 1)
    base = (bj // CAP) * PAD + lax.rem(bj, CAP)
    put_x = jnp.where(bi == base, 1.0, 0.0).astype(BF16)
    put_dot = jnp.where(bi == base + CAP, 1.0, 0.0).astype(BF16)
    once = jnp.where(x == 0, 1.0, 0.0)
    for g in range(n_dev // grp):
        span = pl.ds(g * grp * CAP, grp * CAP)
        mine = jnp.broadcast_to(dots[span] * once, (grp * CAP, depth)).astype(BF16)
        back = jnp.dot(put_x, dx[span].astype(BF16), preferred_element_type=F32)
        back = back + jnp.dot(put_dot, mine, preferred_element_type=F32)
        send2[g * grp : (g + 1) * grp] = back.astype(BF16).reshape(grp, PAD, depth)

    def give(j, _):
        d = lax.rem(me + j, n_dev)
        pltpu.make_async_remote_copy(
            src_ref=send2.at[d], dst_ref=recv2.at[me], send_sem=r_send, recv_sem=r_recv,
            device_id=(d // n_ep, lax.rem(d, n_ep)), device_id_type=MESH,
        ).start()
        return 0

    lax.fori_loop(1, n_dev, give, 0)
    recv2[me] = send2[me]
    everyone2 = recv2.at[pl.ds(0, n_dev - 1)]
    pltpu.make_async_copy(everyone2, everyone2, r_recv).wait()

    route = [jnp.zeros((1, 1), F32) for _ in range(EXP_WIN * CAP)]
    for g in range(n_fsdp):
        grad = jnp.zeros((n_tok, depth), F32)
        for k in range(EXP_WIN):
            acc = recv2[g * n_ep + k * blocks].astype(F32)
            for b in range(1, blocks):
                acc = acc + recv2[g * n_ep + k * blocks + b].astype(F32)
            for c in range(CAP):
                pick = jnp.where(slot_col[k] == c, member_col[k], 0.0)
                grad = grad + pick * acc[c : c + 1, :]
                route[k * CAP + c] = route[k * CAP + c] + acc[CAP + c : CAP + c + 1, 0:1]
        gt_ref[:, g * depth : (g + 1) * depth] = grad.astype(BF16)
    which = iota((n_tok, EXP_WIN), 1)
    out = jnp.zeros((n_tok, EXP_WIN), F32)
    for k in range(EXP_WIN):
        for c in range(CAP):
            pick = jnp.where(slot_col[k] == c, member_col[k], 0.0)
            out = out + jnp.where(which == k, pick * route[k * CAP + c], 0.0)
    rd_ref[...] = out

    pltpu.make_async_copy(everyone, everyone, d_send).wait()
    pltpu.make_async_copy(everyone2, everyone2, r_send).wait()
    for k in range(chunks):
        copy_a(k).wait_send()
        copy_c(k).wait_send()
        for j in range(1, n_x):
            copy_b(k, j).wait_send()
        for slot, h in enumerate((core, 1 - core)):
            for c in stores(h, k, slot):
                c.wait()


def body(n_fsdp, n_ep, tokens, cotangent, routes, logits, w_gate, w_up, w_down):
    n_tok, model = tokens.shape
    depth, width = w_gate.shape
    n_dev = n_fsdp * n_ep
    n_x = n_fsdp // CORES
    rows = n_dev * CAP
    half = width // CORES
    chunks = max(1, min(CHUNKS, half // 128))
    w = half // chunks
    vmem = pl.BlockSpec(memory_space=pltpu.VMEM)
    hbm = pl.BlockSpec(memory_space=pl.ANY)
    dma = pltpu.SemaphoreType.DMA
    return pl.pallas_call(
        functools.partial(kernel, n_fsdp, n_ep, chunks),
        out_shape=(
            jax.ShapeDtypeStruct((n_tok, model), BF16),
            jax.ShapeDtypeStruct((n_tok, EXP_WIN), F32),
            jax.ShapeDtypeStruct(logits.shape, F32),
            jax.ShapeDtypeStruct(w_gate.shape, BF16),
            jax.ShapeDtypeStruct(w_up.shape, BF16),
            jax.ShapeDtypeStruct(w_down.shape, BF16),
        ),
        in_specs=[vmem] * 4 + [hbm] * 3,
        out_specs=[vmem] * 3 + [hbm] * 3,
        scratch_shapes=[
            pltpu.VMEM(w_gate.shape, BF16),
            pltpu.VMEM(w_up.shape, BF16),
            pltpu.VMEM(w_down.shape, BF16),
            pltpu.VMEM(w_gate.shape, BF16),
            pltpu.VMEM(w_up.shape, BF16),
            pltpu.VMEM(w_down.shape, BF16),
            pltpu.VMEM((EXP_WIN, n_fsdp, PAD, depth), BF16),
            pltpu.VMEM((n_dev, PAD, depth), BF16),
            pltpu.VMEM((rows, depth), BF16),
            pltpu.VMEM((rows, depth), BF16),
            pltpu.VMEM((chunks, 3, rows, w), F32),
            pltpu.VMEM((chunks, 3, rows, w), BF16),
            pltpu.VMEM((chunks, 3, rows, w), BF16),
            pltpu.VMEM((chunks, 3, rows, w), BF16),
            pltpu.VMEM((chunks, n_x - 1, 3, rows, w), BF16),
            pltpu.VMEM((chunks, 3, rows, w), BF16),
            pltpu.VMEM((chunks, 3, rows, w), BF16),
            pltpu.VMEM((rows, depth), F32),
            pltpu.VMEM((rows, 1), F32),
            pltpu.VMEM((n_dev, PAD, depth), BF16),
            pltpu.VMEM((n_dev, PAD, depth), BF16),
            dma((3,)),
            dma((chunks, CORES, 3)),
            dma,
            dma,
            dma((chunks,)),
            dma((chunks,)),
            dma((chunks, n_x - 1)),
            dma((chunks, n_x - 1)),
            dma((chunks,)),
            dma((chunks,)),
            dma,
            dma,
        ],
        compiler_params=pltpu.CompilerParams(
            collective_id=0, has_side_effects=True, vmem_limit_bytes=62 * 1024 * 1024
        ),
    )(tokens, cotangent, routes, logits, w_gate, w_up, w_down)


def solution(mesh):
    in_specs = (
        P(("fsdp", "ep"), None),
        P(("fsdp", "ep"), None),
        P(("fsdp", "ep"), None),
        P(("fsdp", "ep"), None),
        P("fsdp", "ep"),
        P("fsdp", "ep"),
        P("ep", "fsdp"),
    )
    out_specs = (
        P(("fsdp", "ep"), None),
        P(("fsdp", "ep"), None),
        P(("fsdp", "ep"), None),
        P("fsdp", "ep"),
        P("fsdp", "ep"),
        P("ep", "fsdp"),
    )
    step = functools.partial(body, mesh.shape["fsdp"], mesh.shape["ep"])
    return jax.shard_map(step, mesh=mesh, in_specs=in_specs, out_specs=out_specs, check_vma=False)
```

time: 426 us -> 56.3 us (0.13)
  waiting for transfers between devices: 265 us -> 0 us
  matrix products: 46.1 us -> 0 us
  Pallas kernels: 0 us -> 43 us
  blocking collectives: 39.6 us -> 0 us
  other arithmetic: 22.6 us -> 0 us
  starting transfers between devices: 22 us -> 0 us
  between operations: 13.9 us -> 0.64 us
    all_gather x3 -> x0, waiting for transfers between devices: 143 us -> none  [the longest x1 55.3 us: body(): lax.all_gather(w_down, 'fsdp', axis=1, tiled=True)]
    reduce_scatter x1 -> x0, waiting for transfers between devices: 101 us -> none  [body(): lax.psum_scatter(jnp.concatenate([lax.dot_general(rows_x, gate_grad, cont...]
    dot_general x13 -> x0, matrix products: 46.1 us -> none  [the longest x1 6.05 us: body(): lax.dot_general(gate_grad, gate_full, contract_last, preferred_element_ty...]
    pallas_call x0 -> x1, Pallas kernels: none -> 43 us  [body(): pl.pallas_call(functools.partial(kernel, n_fsdp, n_ep, chunks), out_shape...]
    psum x1 -> x0, blocking collectives: 39.6 us -> none  [body(): total_counts = lax.psum(local_counts, ('fsdp', 'ep'))]
    all_to_all x4 -> x0, starting transfers between devices: 21.9 us -> none  [the longest x1 7.31 us: body(): lax.all_to_all(send_tokens, 'ep', split_axis=0, concat_axis=0, tiled=True)]
    all_to_all x4 -> x0, waiting for transfers between devices: 19.6 us -> none  [the longest x1 7.14 us: body(): lax.all_to_all(send_grads, 'ep', split_axis=0, concat_axis=0, tiled=True)]
    concatenate x1 -> x0, other arithmetic: 18 us -> none  [body(): jnp.concatenate([lax.dot_general(rows_x, gate_grad, contract_first, prefe...]
  transfers between devices with their start and end apart: 8 -> 0, of which waited for: 7 -> 0; matrix products, arithmetic and copies ran while one was open for 7% -> 0% of each run, Pallas kernels for 0% -> 0%
where the time goes in v1:
time: 56.3 us; the launch traced here: 55.9 us
  Pallas kernels  43 us (76%)
  local copies, waits for them, and re-layouts  12.3 us (22%)
  between operations  0.64 us (1%)
    pallas_call x1, Pallas kernels, body(): pl.pallas_call(functools.partial(kernel, n_fsdp, n_ep, chunks), out_shape...  43 us
    unnamed x10, local copies, waits for them, and re-layouts  11 us
    pallas_call x1, local copies, waits for them, and re-layouts, body(): pl.pallas_call(functools.partial(kernel, n_fsdp, n_ep, chunks), out_shape...  1.31 us

profile of v1, /device:TPU:0, one launch (start us, length us, event | category | flops | bytes accessed | tf_op | source)
XLA Modules:
  0.0 55.9 jit_solution(16695020277646190520)
XLA Ops:
  0.6 1.3 %copy.13.routes_ref = s32[8,2]{1,0:T(8,128)} copy(s32[8,2]{0,1:T(2,128)} %param.9) | data formatting | bytes 128 | tf_op args[2]
  2.0 43.0 %shard_map.118 = (bf16[8,2048]{1,0:T(8,128)(2,1)}, f32[8,2]{1,0:T(8,128)}, f32[8,8]{1,0:T(8,128)}, bf16[512,2048]{1,0:T(8,128)(2,1)}, bf16[512,2048]{1,0:T(8,128)(2,1)}, /*index=5*/bf16[2048,512]{1,0:T(8,128)(2,1)}) custom-call(bf16[8,2048]{1,0:T(8,128)(2,1)} %tok_ref.1, bf16[8,2048]{1,0:T(8,128)(2,1)} %cot_ref.1, s32[8,2]{1,0:T(8,128)} %copy.13.routes_ref, ...), custom_call_target="tpu_custom_call" | custom-call | tf_op jit(solution)/shard_map/pallas_call | solution.py:315
  44.9 1.3 %copy.14 = f32[8,2]{0,1:T(2,128)} copy(f32[8,2]{1,0:T(8,128)} %get-tuple-element.7) | data formatting | bytes 128 | tf_op jit(solution)/shard_map/pallas_call | solution.py:315
  46.3 1.4 %copy.20 = bf16[8,2048]{1,0:T(8,128)(2,1)} copy(bf16[8,2048]{1,0:T(8,128)(2,1)} %get-tuple-element.18) | data formatting | bytes 65536
  47.6 1.3 %copy.21 = f32[8,8]{1,0:T(8,128)} copy(f32[8,8]{1,0:T(8,128)} %get-tuple-element.20) | data formatting | bytes 512
  48.9 0.0 copy-start.1
  48.9 3.3 %copy.22 = bf16[512,2048]{1,0:T(8,128)(2,1)} copy(bf16[512,2048]{1,0:T(8,128)(2,1)} %get-tuple-element.21) | data formatting | bytes 4194304
  52.2 0.0 copy-done.1
  52.2 0.0 copy-start
  52.2 1.3 %copy.23 = bf16[512,2048]{1,0:T(8,128)(2,1)} copy(bf16[512,2048]{1,0:T(8,128)(2,1)S(1)} %copy-done.1) | data formatting | bytes 4194304
  53.5 1.0 %copy-done = bf16[2048,512]{1,0:T(8,128)(2,1)S(1)} copy-done((bf16[2048,512]{1,0:T(8,128)(2,1)S(1)}, bf16[2048,512]{1,0:T(8,128)(2,1)}, u32[]{:S(2)}) %copy-start) | copy-done | bytes 2097176
  54.6 1.3 %copy.24 = bf16[2048,512]{1,0:T(8,128)(2,1)} copy(bf16[2048,512]{1,0:T(8,128)(2,1)S(1)} %copy-done) | data formatting | bytes 4194304
Async XLA Ops:
  48.9 3.3 %copy-start.1 = (bf16[512,2048]{1,0:T(8,128)(2,1)S(1)}, bf16[512,2048]{1,0:T(8,128)(2,1)}, u32[]{:S(2)}) copy-start(bf16[512,2048]{1,0:T(8,128)(2,1)} %get-tuple-element.22) | copy-start | bytes 6291460
  52.2 2.3 %copy-start = (bf16[2048,512]{1,0:T(8,128)(2,1)S(1)}, bf16[2048,512]{1,0:T(8,128)(2,1)}, u32[]{:S(2)}) copy-start(bf16[2048,512]{1,0:T(8,128)(2,1)} %get-tuple-element.23) | copy-start | bytes 6291460

commit v2 on v1

--- a/solution.py
+++ b/solution.py
@@ -26,11 +26,11 @@
 def kernel(
     n_fsdp, n_ep, chunks,
     tok_ref, cot_ref, routes_ref, logits_ref, wg_hbm, wu_hbm, wd_hbm,
-    gt_ref, rd_ref, aux_ref, gg_hbm, gu_hbm, gd_hbm,
-    wg, wu, wd, og, ou, od,
+    gt_ref, rd_ref, aux_ref, x_hbm, dy_hbm, acts_hbm,
+    wg, wu, wd,
     send1, recv1, rows_x, rows_dy,
     own_a, send_a, recv_a, send_b, recv_b, acts, recv_c, dx, dots, send2, recv2,
-    w_sem, o_sem, d_send, d_recv, a_send, a_recv, b_send, b_recv, c_send, c_recv, r_send, r_recv,
+    w_sem, o_sem, x_sem, d_send, d_recv, a_send, a_recv, b_send, b_recv, c_send, c_recv, r_send, r_recv,
 ):
     n_dev = n_fsdp * n_ep
     n_x = n_fsdp // CORES
@@ -61,14 +61,16 @@
     routes = routes_ref[...]
     logits = logits_ref[...]
     n_tok, n_exp = logits.shape
-    r0, r1 = routes[:, 0:1], routes[:, 1:2]
+    ti, tj = iota((n_tok, n_tok), 0), iota((n_tok, n_tok), 1)
+    r0, r1 = (
+        jnp.sum(jnp.where(ti == tj, routes[k : k + 1, :], 0), axis=1, keepdims=True) for k in range(2)
+    )
     experts = iota((n_tok, n_exp), 1)
     c0 = jnp.sum(jnp.where(experts == r0, logits, 0.0), axis=1, keepdims=True)
     c1 = jnp.sum(jnp.where(experts == r1, logits, 0.0), axis=1, keepdims=True)
     top = jnp.maximum(c0, c1)
     e0, e1 = jnp.exp(c0 - top), jnp.exp(c1 - top)
     p0, p1 = e0 / (e0 + e1), e1 / (e0 + e1)
-    ti, tj = iota((n_tok, n_tok), 0), iota((n_tok, n_tok), 1)
     ci = iota((PAD, n_tok), 0)
     lanes = iota((n_tok, depth), 1)
     counts = jnp.sum(
@@ -76,7 +78,7 @@
     )
     tok = tok_ref[...]
     cot = cot_ref[...].astype(F32)
-    member_col, slot_col = [], []
+    member_col, slot_col, member_row, slot_line = [], [], [], []
     row_id = iota((PAD, depth), 0)
     for k in range(EXP_WIN):
         m0, m1 = jnp.where(r0 == k, 1.0, 0.0), jnp.where(r1 == k, 1.0, 0.0)
@@ -86,6 +88,8 @@
         slot_row = jnp.sum(jnp.where(ti < tj, col, 0.0), axis=0, keepdims=True)
         slot_col.append(jnp.sum(jnp.where(tj < ti, row, 0.0), axis=1, keepdims=True))
         member_col.append(col)
+        member_row.append(row)
+        slot_line.append(slot_row)
         cf = ci.astype(F32)
         sel_a = jnp.where((cf == slot_row) & (ci < CAP), row, 0.0).astype(BF16)
         sel_b = jnp.where((cf - CAP == slot_row) & (ci < 2 * CAP), row, 0.0).astype(BF16)
@@ -192,35 +196,25 @@
         acts[k, 2] = hidden
         copy_c(k).start()
 
-    outs = ((og, gg_hbm), (ou, gu_hbm))
-
     def grads(h, k, source):
         cols = columns(h, k)
-        xs, dys = rows_x[...], rows_dy[...]
-        gate_grad, up_grad, hidden = source[k, 0], source[k, 1], source[k, 2]
-        part = lax.dot_general(gate_grad, wg[:, cols], LAST, preferred_element_type=F32)
-        part = part + lax.dot_general(up_grad, wu[:, cols], LAST, preferred_element_type=F32)
-        og[:, cols] = lax.dot_general(xs, gate_grad, FIRST, preferred_element_type=F32).astype(BF16)
-        ou[:, cols] = lax.dot_general(xs, up_grad, FIRST, preferred_element_type=F32).astype(BF16)
-        od[cols, :] = lax.dot_general(hidden, dys, FIRST, preferred_element_type=F32).astype(BF16)
-        return part
-
-    def stores(h, k, slot):
-        cols = columns(h, k)
-        return [
-            pltpu.make_async_copy(og.at[:, cols], gg_hbm.at[:, cols], o_sem.at[k, slot, 0]),
-            pltpu.make_async_copy(ou.at[:, cols], gu_hbm.at[:, cols], o_sem.at[k, slot, 1]),
-            pltpu.make_async_copy(od.at[cols, :], gd_hbm.at[cols, :], o_sem.at[k, slot, 2]),
-        ]
+        part = lax.dot_general(source[k, 0], wg[:, cols], LAST, preferred_element_type=F32)
+        return part + lax.dot_general(source[k, 1], wu[:, cols], LAST, preferred_element_type=F32)
+
+    def store(h, k, slot, source):
+        return pltpu.make_async_copy(source.at[k], acts_hbm.at[h, k], o_sem.at[k, slot])
+
+    row_stores = [
+        pltpu.make_async_copy(rows_x, x_hbm, x_sem.at[0]),
+        pltpu.make_async_copy(rows_dy, dy_hbm, x_sem.at[1]),
+    ]
 
     def stage4(k):
         part = grads(core, k, acts)
-        for c in stores(core, k, 0):
-            c.start()
+        store(core, k, 0, acts).start()
         copy_c(k).wait_recv()
         part = part + grads(1 - core, k, recv_c)
-        for c in stores(1 - core, k, 1):
-            c.start()
+        store(1 - core, k, 1, recv_c).start()
         dx[...] = part if k == 0 else dx[...] + part
 
     for c in loads:
@@ -230,6 +224,9 @@
         stage1(k)
         stage2(k - 1)
     stage2(chunks - 1)
+
+    for c in row_stores:
+        c.start()
 
     count = total[0:1, 0:n_exp]
     target = n_exp * (count / jnp.sum(count, axis=1, keepdims=True))
@@ -280,11 +277,11 @@
                 grad = grad + pick * acc[c : c + 1, :]
                 route[k * CAP + c] = route[k * CAP + c] + acc[CAP + c : CAP + c + 1, 0:1]
         gt_ref[:, g * depth : (g + 1) * depth] = grad.astype(BF16)
-    which = iota((n_tok, EXP_WIN), 1)
-    out = jnp.zeros((n_tok, EXP_WIN), F32)
+    which = iota((EXP_WIN, n_tok), 0)
+    out = jnp.zeros((EXP_WIN, n_tok), F32)
     for k in range(EXP_WIN):
         for c in range(CAP):
-            pick = jnp.where(slot_col[k] == c, member_col[k], 0.0)
+            pick = jnp.where(slot_line[k] == c, member_row[k], 0.0)
             out = out + jnp.where(which == k, pick * route[k * CAP + c], 0.0)
     rd_ref[...] = out
 
@@ -295,9 +292,23 @@
         copy_c(k).wait_send()
         for j in range(1, n_x):
             copy_b(k, j).wait_send()
-        for slot, h in enumerate((core, 1 - core)):
-            for c in stores(h, k, slot):
-                c.wait()
+        store(core, k, 0, acts).wait()
+        store(1 - core, k, 1, recv_c).wait()
+    for c in row_stores:
+        c.wait()
+
+
+def weight_kernel(x_ref, dy_ref, acts_ref, gt_in, rd_in, aux_in, gt_ref, rd_ref, aux_ref, og, ou, od):
+    xs, dys = x_ref[...], dy_ref[...]
+    og[...] = lax.dot_general(xs, acts_ref[0], FIRST, preferred_element_type=F32).astype(BF16)
+    ou[...] = lax.dot_general(xs, acts_ref[1], FIRST, preferred_element_type=F32).astype(BF16)
+    od[...] = lax.dot_general(acts_ref[2], dys, FIRST, preferred_element_type=F32).astype(BF16)
+
+    @pl.when(pl.program_id(0) == 0)
+    def _():
+        gt_ref[...] = gt_in[...]
+        rd_ref[...] = rd_in[...]
+        aux_ref[...] = aux_in[...]
 
 
 def body(n_fsdp, n_ep, tokens, cotangent, routes, logits, w_gate, w_up, w_down):
@@ -312,22 +323,19 @@
     vmem = pl.BlockSpec(memory_space=pltpu.VMEM)
     hbm = pl.BlockSpec(memory_space=pl.ANY)
     dma = pltpu.SemaphoreType.DMA
-    return pl.pallas_call(
+    small_x, small_r, small_a, all_x, all_dy, all_acts = pl.pallas_call(
         functools.partial(kernel, n_fsdp, n_ep, chunks),
         out_shape=(
             jax.ShapeDtypeStruct((n_tok, model), BF16),
-            jax.ShapeDtypeStruct((n_tok, EXP_WIN), F32),
+            jax.ShapeDtypeStruct((EXP_WIN, n_tok), F32),
             jax.ShapeDtypeStruct(logits.shape, F32),
-            jax.ShapeDtypeStruct(w_gate.shape, BF16),
-            jax.ShapeDtypeStruct(w_up.shape, BF16),
-            jax.ShapeDtypeStruct(w_down.shape, BF16),
+            jax.ShapeDtypeStruct((rows, depth), BF16),
+            jax.ShapeDtypeStruct((rows, depth), BF16),
+            jax.ShapeDtypeStruct((CORES, chunks, 3, rows, w), BF16),
         ),
         in_specs=[vmem] * 4 + [hbm] * 3,
         out_specs=[vmem] * 3 + [hbm] * 3,
         scratch_shapes=[
-            pltpu.VMEM(w_gate.shape, BF16),
-            pltpu.VMEM(w_up.shape, BF16),
-            pltpu.VMEM(w_down.shape, BF16),
             pltpu.VMEM(w_gate.shape, BF16),
             pltpu.VMEM(w_up.shape, BF16),
             pltpu.VMEM(w_down.shape, BF16),
@@ -347,7 +355,8 @@
             pltpu.VMEM((n_dev, PAD, depth), BF16),
             pltpu.VMEM((n_dev, PAD, depth), BF16),
             dma((3,)),
-            dma((chunks, CORES, 3)),
+            dma((chunks, CORES)),
+            dma((2,)),
             dma,
             dma,
             dma((chunks,)),
@@ -362,7 +371,42 @@
         compiler_params=pltpu.CompilerParams(
             collective_id=0, has_side_effects=True, vmem_limit_bytes=62 * 1024 * 1024
         ),
-    )(tokens, cotangent, routes, logits, w_gate, w_up, w_down)
+    )(tokens, cotangent, jnp.transpose(routes), logits, w_gate, w_up, w_down)
+    step = min(256, w)
+    per = w // step
+
+    def same(i):
+        return (0, 0)
+
+    def whole(a):
+        return pl.BlockSpec(a.shape, same)
+
+    smalls = [whole(small_x), whole(small_r), whole(small_a)]
+    cols = pl.BlockSpec((depth, step), lambda i: (0, i))
+    out = pl.pallas_call(
+        weight_kernel,
+        grid=(width // step,),
+        out_shape=(
+            jax.ShapeDtypeStruct(small_x.shape, BF16),
+            jax.ShapeDtypeStruct(small_r.shape, F32),
+            jax.ShapeDtypeStruct(small_a.shape, F32),
+            jax.ShapeDtypeStruct(w_gate.shape, BF16),
+            jax.ShapeDtypeStruct(w_up.shape, BF16),
+            jax.ShapeDtypeStruct(w_down.shape, BF16),
+        ),
+        in_specs=[
+            whole(all_x),
+            whole(all_dy),
+            pl.BlockSpec(
+                (None, None, 3, rows, step),
+                lambda i: (i // (chunks * per), lax.rem(i // per, chunks), 0, 0, lax.rem(i, per)),
+            ),
+        ]
+        + smalls,
+        out_specs=smalls + [cols, cols, pl.BlockSpec((step, depth), lambda i: (i, 0))],
+        compiler_params=pltpu.CompilerParams(dimension_semantics=("arbitrary",)),
+    )(all_x, all_dy, all_acts, small_x, small_r, small_a)
+    return (out[0], jnp.transpose(out[1])) + tuple(out[2:])
 
 
 def solution(mesh):

time: 56.3 us -> 51.3 us (0.911)
  local copies, waits for them, and re-layouts: 12.3 us -> 0 us
  Pallas kernels: 43 us -> 50.3 us
    unnamed x10 -> x0, local copies, waits for them, and re-layouts: 11 us -> none
    pallas_call x0 -> x1, Pallas kernels: none -> 7.74 us  [body(): pl.pallas_call(weight_kernel, grid=(width // step,), out_shape=(jax.Shape...]
    pallas_call x1 -> x0, local copies, waits for them, and re-layouts: 1.31 us -> none  [body(): pl.pallas_call(functools.partial(kernel, n_fsdp, n_ep, chunks), out_shape...]
where the time goes in v2:
time: 51.3 us; the launch traced here: 50.9 us
  Pallas kernels  50.3 us (98%)
  between operations  0.64 us (1%)
    pallas_call x1, Pallas kernels, body(): pl.pallas_call(functools.partial(kernel, n_fsdp, n_ep, chunks), out_shape...  42.5 us
    pallas_call x1, Pallas kernels, body(): pl.pallas_call(weight_kernel, grid=(width // step,), out_shape=(jax.Shape...  7.74 us

profile of v2, /device:TPU:0, one launch (start us, length us, event | category | flops | bytes accessed | tf_op | source)
XLA Modules:
  0.0 50.9 jit_solution(18438360650398015567)
XLA Ops:
  0.6 42.5 %shard_map.118 = (bf16[8,2048]{1,0:T(8,128)(2,1)}, f32[2,8]{1,0:T(2,128)}, f32[8,8]{1,0:T(8,128)}, bf16[96,512]{1,0:T(8,128)(2,1)}, bf16[96,512]{1,0:T(8,128)(2,1)}, /*index=5*/bf16[2,4,3,96,256]{4,3,2,1,0:T(8,128)(2,1)}) custom-call(bf16[8,2048]{1,0:T(8,128)(2,1)} %tok_ref.1, bf16[8,2048]{1,0:T(8,128)(2,1)} %cot_ref.1, s32[2,8]{1,0:T(2,128)} %bitcast.2, ...), custom_call_target="tpu_custom_call" | custom-call | tf_op jit(solution)/shard_map/pallas_call | solution.py:326
  43.2 7.7 %shard_map.119 = (bf16[8,2048]{1,0:T(8,128)(2,1)}, f32[2,8]{1,0:T(2,128)}, f32[8,8]{1,0:T(8,128)}, bf16[512,2048]{1,0:T(8,128)(2,1)}, bf16[512,2048]{1,0:T(8,128)(2,1)}, /*index=5*/bf16[2048,512]{1,0:T(8,128)(2,1)}) custom-call(bf16[96,512]{1,0:T(8,128)(2,1)} %get-tuple-element.18.x_ref, bf16[96,512]{1,0:T(8,128)(2,1)} %get-tuple-element.19.dy_ref, ...), custom_call_target="tpu_custom_call" | custom-call | tf_op jit(solution)/shard_map/pallas_call | solution.py:386

commit v3 on v2

--- a/solution.py
+++ b/solution.py
@@ -12,6 +12,7 @@
 PAD = 8
 CORES = 2
 CHUNKS = 4
+GROUPS = 2
 LAST = (((1,), (1,)), ((), ()))
 FIRST = (((0,), (0,)), ((), ()))
 F32 = jnp.float32
@@ -42,6 +43,13 @@
     depth, width = wg.shape
     half = width // CORES
     w = half // chunks
+    ring = n_ep // GROUPS
+    size = n_fsdp * ring
+    span_rows = size * CAP
+    place = f * ring + e // GROUPS
+
+    def peer(t, i):
+        return i // ring, lax.rem(i, ring) * GROUPS + lax.rem(e + t, GROUPS)
 
     barrier = pltpu.get_barrier_semaphore()
 
@@ -102,21 +110,21 @@
 
     pl.semaphore_wait(barrier, n_dev - 1)
 
-    def push(j, _):
-        d = lax.rem(me + j, n_dev)
-        df, de = d // n_ep, lax.rem(d, n_ep)
-        pltpu.make_async_remote_copy(
-            src_ref=send1.at[de // blocks, df], dst_ref=recv1.at[me], send_sem=d_send, recv_sem=d_recv,
-            device_id=(df, de), device_id_type=MESH,
-        ).start()
-        return 0
-
-    lax.fori_loop(1, n_dev, push, 0)
-    recv1[me] = send1[e // blocks, f]
-    everyone = recv1.at[pl.ds(0, n_dev - 1)]
-    pltpu.make_async_copy(everyone, everyone, d_recv).wait()
-
-    grp = min(32, n_dev)
+    recv1[place] = send1[e // blocks, f]
+    for t in range(GROUPS):
+        back_t = (GROUPS - t) % GROUPS
+
+        def push(j, _, t=t, back_t=back_t):
+            df, de = peer(t, lax.rem(place + j, size))
+            pltpu.make_async_remote_copy(
+                src_ref=send1.at[de // blocks, df], dst_ref=recv1.at[back_t * size + place],
+                send_sem=d_send, recv_sem=d_recv.at[back_t], device_id=(df, de), device_id_type=MESH,
+            ).start()
+            return 0
+
+        lax.fori_loop(1 if t == 0 else 0, size, push, 0)
+
+    grp = min(16, size)
     si, sj = iota((grp * CAP, grp * PAD), 0), iota((grp * CAP, grp * PAD), 1)
     base = (si // CAP) * PAD + lax.rem(si, CAP)
     pick_x = jnp.where(sj == base, 1.0, 0.0).astype(BF16)
@@ -124,13 +132,17 @@
     pick_c = jnp.where(
         lax.rem(iota((8, grp * PAD), 1), PAD) == 2 * CAP, 1.0, 0.0
     ).astype(BF16)
-    total = jnp.zeros((8, depth), F32)
-    for g in range(n_dev // grp):
-        came = recv1[g * grp : (g + 1) * grp].reshape(grp * PAD, depth)
-        span = pl.ds(g * grp * CAP, grp * CAP)
-        rows_x[span] = jnp.dot(pick_x, came, preferred_element_type=F32).astype(BF16)
-        rows_dy[span] = jnp.dot(pick_dy, came, preferred_element_type=F32).astype(BF16)
-        total = total + jnp.dot(pick_c, came, preferred_element_type=F32)
+
+    def prepare(t, total):
+        landed = recv1.at[pl.ds(t * size, size - 1 if t == 0 else size)]
+        pltpu.make_async_copy(landed, landed, d_recv.at[t]).wait()
+        for g in range(t * size // grp, (t + 1) * size // grp):
+            came = recv1[g * grp : (g + 1) * grp].reshape(grp * PAD, depth)
+            span = pl.ds(g * grp * CAP, grp * CAP)
+            rows_x[span] = jnp.dot(pick_x, came, preferred_element_type=F32).astype(BF16)
+            rows_dy[span] = jnp.dot(pick_dy, came, preferred_element_type=F32).astype(BF16)
+            total = total + jnp.dot(pick_c, came, preferred_element_type=F32)
+        return total
 
     def copy_a(k):
         return pltpu.make_async_remote_copy(
@@ -154,9 +166,12 @@
     def columns(h, k):
         return pl.ds(pl.multiple_of(h * half + k * w, w), w)
 
-    def partials(h, k):
-        cols = columns(h, k)
-        xs, dys = rows_x[...], rows_dy[...]
+    def group(u):
+        return pl.ds(u // chunks * span_rows, span_rows)
+
+    def partials(h, u):
+        cols = columns(h, u % chunks)
+        xs, dys = rows_x[group(u)], rows_dy[group(u)]
         yield jnp.dot(xs, wg[:, cols], preferred_element_type=F32)
         yield jnp.dot(xs, wu[:, cols], preferred_element_type=F32)
         yield lax.dot_general(dys, wd[cols, :], LAST, preferred_element_type=F32)
@@ -190,19 +205,19 @@
         active = gate_pre * sigma
         hidden = (active * up_pre).astype(BF16)
         dot = jnp.sum(hidden.astype(F32) * hidden_grad, axis=1, keepdims=True)
-        dots[...] = dot if k == 0 else dots[...] + dot
+        dots[group(k)] = dot if k % chunks == 0 else dots[group(k)] + dot
         acts[k, 0] = (hidden_grad * up_pre * sigma * (1.0 + gate_pre * (1.0 - sigma))).astype(BF16)
         acts[k, 1] = (hidden_grad * active).astype(BF16)
         acts[k, 2] = hidden
         copy_c(k).start()
 
     def grads(h, k, source):
-        cols = columns(h, k)
+        cols = columns(h, k % chunks)
         part = lax.dot_general(source[k, 0], wg[:, cols], LAST, preferred_element_type=F32)
         return part + lax.dot_general(source[k, 1], wu[:, cols], LAST, preferred_element_type=F32)
 
     def store(h, k, slot, source):
-        return pltpu.make_async_copy(source.at[k], acts_hbm.at[h, k], o_sem.at[k, slot])
+        return pltpu.make_async_copy(source.at[k], acts_hbm.at[h, k % chunks, :, group(k), :], o_sem.at[k, slot])
 
     row_stores = [
         pltpu.make_async_copy(rows_x, x_hbm, x_sem.at[0]),
@@ -215,15 +230,18 @@
         copy_c(k).wait_recv()
         part = part + grads(1 - core, k, recv_c)
         store(1 - core, k, 1, recv_c).start()
-        dx[...] = part if k == 0 else dx[...] + part
+        dx[group(k)] = part if k % chunks == 0 else dx[group(k)] + part
 
     for c in loads:
         c.wait()
-    stage1(0)
-    for k in range(1, chunks):
-        stage1(k)
-        stage2(k - 1)
-    stage2(chunks - 1)
+    total = jnp.zeros((8, depth), F32)
+    for t in range(GROUPS):
+        total = prepare(t, total)
+        for k in range(t * chunks, (t + 1) * chunks):
+            stage1(k)
+            if k > 0:
+                stage2(k - 1)
+    stage2(GROUPS * chunks - 1)
 
     for c in row_stores:
         c.start()
@@ -234,34 +252,41 @@
     probs = raised / jnp.sum(raised, axis=1, keepdims=True)
     aux_ref[...] = probs * (target - jnp.sum(probs * target, axis=1, keepdims=True))
 
-    stage3(0)
-    for k in range(1, chunks):
-        stage3(k)
-        stage4(k - 1)
-    stage4(chunks - 1)
-
     bi, bj = iota((grp * PAD, grp * CAP), 0), iota((grp * PAD, grp * CAP), 1)
     base = (bj // CAP) * PAD + lax.rem(bj, CAP)
     put_x = jnp.where(bi == base, 1.0, 0.0).astype(BF16)
     put_dot = jnp.where(bi == base + CAP, 1.0, 0.0).astype(BF16)
     once = jnp.where(x == 0, 1.0, 0.0)
-    for g in range(n_dev // grp):
-        span = pl.ds(g * grp * CAP, grp * CAP)
-        mine = jnp.broadcast_to(dots[span] * once, (grp * CAP, depth)).astype(BF16)
-        back = jnp.dot(put_x, dx[span].astype(BF16), preferred_element_type=F32)
-        back = back + jnp.dot(put_dot, mine, preferred_element_type=F32)
-        send2[g * grp : (g + 1) * grp] = back.astype(BF16).reshape(grp, PAD, depth)
-
-    def give(j, _):
-        d = lax.rem(me + j, n_dev)
-        pltpu.make_async_remote_copy(
-            src_ref=send2.at[d], dst_ref=recv2.at[me], send_sem=r_send, recv_sem=r_recv,
-            device_id=(d // n_ep, lax.rem(d, n_ep)), device_id_type=MESH,
-        ).start()
-        return 0
-
-    lax.fori_loop(1, n_dev, give, 0)
-    recv2[me] = send2[me]
+
+    def give_back(t):
+        for g in range(t * size // grp, (t + 1) * size // grp):
+            span = pl.ds(g * grp * CAP, grp * CAP)
+            mine = jnp.broadcast_to(dots[span] * once, (grp * CAP, depth)).astype(BF16)
+            back = jnp.dot(put_x, dx[span].astype(BF16), preferred_element_type=F32)
+            back = back + jnp.dot(put_dot, mine, preferred_element_type=F32)
+            send2[g * grp : (g + 1) * grp] = back.astype(BF16).reshape(grp, PAD, depth)
+
+        def give(j, _):
+            i = lax.rem(place + j, size)
+            pltpu.make_async_remote_copy(
+                src_ref=send2.at[t * size + i], dst_ref=recv2.at[me], send_sem=r_send, recv_sem=r_recv,
+                device_id=peer(t, i), device_id_type=MESH,
+            ).start()
+            return 0
+
+        lax.fori_loop(1 if t == 0 else 0, size, give, 0)
+        if t == 0:
+            recv2[me] = send2[place]
+
+    for k in range(GROUPS * chunks):
+        stage3(k)
+        if k > 0:
+            stage4(k - 1)
+            if k % chunks == 0:
+                give_back(k // chunks - 1)
+    stage4(GROUPS * chunks - 1)
+    give_back(GROUPS - 1)
+    everyone = recv1.at[pl.ds(0, n_dev - 1)]
     everyone2 = recv2.at[pl.ds(0, n_dev - 1)]
     pltpu.make_async_copy(everyone2, everyone2, r_recv).wait()
 
@@ -287,7 +312,7 @@
 
     pltpu.make_async_copy(everyone, everyone, d_send).wait()
     pltpu.make_async_copy(everyone2, everyone2, r_send).wait()
-    for k in range(chunks):
+    for k in range(GROUPS * chunks):
         copy_a(k).wait_send()
         copy_c(k).wait_send()
         for j in range(1, n_x):
@@ -320,6 +345,7 @@
     half = width // CORES
     chunks = max(1, min(CHUNKS, half // 128))
     w = half // chunks
+    items, part = GROUPS * chunks, rows // GROUPS
     vmem = pl.BlockSpec(memory_space=pltpu.VMEM)
     hbm = pl.BlockSpec(memory_space=pl.ANY)
     dma = pltpu.SemaphoreType.DMA
@@ -343,28 +369,28 @@
             pltpu.VMEM((n_dev, PAD, depth), BF16),
             pltpu.VMEM((rows, depth), BF16),
             pltpu.VMEM((rows, depth), BF16),
-            pltpu.VMEM((chunks, 3, rows, w), F32),
-            pltpu.VMEM((chunks, 3, rows, w), BF16),
-            pltpu.VMEM((chunks, 3, rows, w), BF16),
-            pltpu.VMEM((chunks, 3, rows, w), BF16),
-            pltpu.VMEM((chunks, n_x - 1, 3, rows, w), BF16),
-            pltpu.VMEM((chunks, 3, rows, w), BF16),
-            pltpu.VMEM((chunks, 3, rows, w), BF16),
+            pltpu.VMEM((items, 3, part, w), F32),
+            pltpu.VMEM((items, 3, part, w), BF16),
+            pltpu.VMEM((items, 3, part, w), BF16),
+            pltpu.VMEM((items, 3, part, w), BF16),
+            pltpu.VMEM((items, n_x - 1, 3, part, w), BF16),
+            pltpu.VMEM((items, 3, part, w), BF16),
+            pltpu.VMEM((items, 3, part, w), BF16),
             pltpu.VMEM((rows, depth), F32),
             pltpu.VMEM((rows, 1), F32),
             pltpu.VMEM((n_dev, PAD, depth), BF16),
             pltpu.VMEM((n_dev, PAD, depth), BF16),
             dma((3,)),
-            dma((chunks, CORES)),
+            dma((items, CORES)),
             dma((2,)),
             dma,
-            dma,
-            dma((chunks,)),
-            dma((chunks,)),
-            dma((chunks, n_x - 1)),
-            dma((chunks, n_x - 1)),
-            dma((chunks,)),
-            dma((chunks,)),
+            dma((GROUPS,)),
+            dma((items,)),
+            dma((items,)),
+            dma((items, n_x - 1)),
+            dma((items, n_x - 1)),
+            dma((items,)),
+            dma((items,)),
             dma,
             dma,
         ],

time: 51.3 us -> 47.7 us (0.930)
  Pallas kernels: 50.3 us -> 46.8 us
    pallas_call x1, Pallas kernels: 42.5 us -> 39 us  [body(): pl.pallas_call(functools.partial(kernel, n_fsdp, n_ep, chunks), out_shape...]
where the time goes in v3:
time: 47.7 us; the launch traced here: 47.4 us
  Pallas kernels  46.8 us (98%)
  between operations  0.64 us (1%)
    pallas_call x1, Pallas kernels, body(): pl.pallas_call(functools.partial(kernel, n_fsdp, n_ep, chunks), out_shape...  39 us
    pallas_call x1, Pallas kernels, body(): pl.pallas_call(weight_kernel, grid=(width // step,), out_shape=(jax.Shape...  7.74 us

profile of v3, /device:TPU:0, one launch (start us, length us, event | category | flops | bytes accessed | tf_op | source)
XLA Modules:
  0.0 47.4 jit_solution(16801375520258609396)
XLA Ops:
  0.6 39.0 %shard_map.118 = (bf16[8,2048]{1,0:T(8,128)(2,1)}, f32[2,8]{1,0:T(2,128)}, f32[8,8]{1,0:T(8,128)}, bf16[96,512]{1,0:T(8,128)(2,1)}, bf16[96,512]{1,0:T(8,128)(2,1)}, /*index=5*/bf16[2,4,3,96,256]{4,3,2,1,0:T(8,128)(2,1)}) custom-call(bf16[8,2048]{1,0:T(8,128)(2,1)} %tok_ref.1, bf16[8,2048]{1,0:T(8,128)(2,1)} %cot_ref.1, s32[2,8]{1,0:T(2,128)} %bitcast.2, ...), custom_call_target="tpu_custom_call" | custom-call | tf_op jit(solution)/shard_map/pallas_call | solution.py:352
  39.7 7.7 %shard_map.119 = (bf16[8,2048]{1,0:T(8,128)(2,1)}, f32[2,8]{1,0:T(2,128)}, f32[8,8]{1,0:T(8,128)}, bf16[512,2048]{1,0:T(8,128)(2,1)}, bf16[512,2048]{1,0:T(8,128)(2,1)}, /*index=5*/bf16[2048,512]{1,0:T(8,128)(2,1)}) custom-call(bf16[96,512]{1,0:T(8,128)(2,1)} %get-tuple-element.18.x_ref, bf16[96,512]{1,0:T(8,128)(2,1)} %get-tuple-element.19.dy_ref, ...), custom_call_target="tpu_custom_call" | custom-call | tf_op jit(solution)/shard_map/pallas_call | solution.py:412

commit v4 on v3

--- a/solution.py
+++ b/solution.py
@@ -325,9 +325,12 @@
 
 def weight_kernel(x_ref, dy_ref, acts_ref, gt_in, rd_in, aux_in, gt_ref, rd_ref, aux_ref, og, ou, od):
     xs, dys = x_ref[...], dy_ref[...]
-    og[...] = lax.dot_general(xs, acts_ref[0], FIRST, preferred_element_type=F32).astype(BF16)
-    ou[...] = lax.dot_general(xs, acts_ref[1], FIRST, preferred_element_type=F32).astype(BF16)
-    od[...] = lax.dot_general(acts_ref[2], dys, FIRST, preferred_element_type=F32).astype(BF16)
+    for p in range(acts_ref.shape[0]):
+        w = acts_ref.shape[3]
+        c = pl.ds(p * w, w)
+        og[:, c] = lax.dot_general(xs, acts_ref[p, 0], FIRST, preferred_element_type=F32).astype(BF16)
+        ou[:, c] = lax.dot_general(xs, acts_ref[p, 1], FIRST, preferred_element_type=F32).astype(BF16)
+        od[c, :] = lax.dot_general(acts_ref[p, 2], dys, FIRST, preferred_element_type=F32).astype(BF16)
 
     @pl.when(pl.program_id(0) == 0)
     def _():
@@ -398,8 +401,9 @@
             collective_id=0, has_side_effects=True, vmem_limit_bytes=62 * 1024 * 1024
         ),
     )(tokens, cotangent, jnp.transpose(routes), logits, w_gate, w_up, w_down)
-    step = min(256, w)
-    per = w // step
+    pair = 2 if chunks % 2 == 0 else 1
+    step = w * pair
+    per = chunks // pair
 
     def same(i):
         return (0, 0)
@@ -424,8 +428,8 @@
             whole(all_x),
             whole(all_dy),
             pl.BlockSpec(
-                (None, None, 3, rows, step),
-                lambda i: (i // (chunks * per), lax.rem(i // per, chunks), 0, 0, lax.rem(i, per)),
+                (None, pair, 3, rows, w),
+                lambda i: (i // per, lax.rem(i, per), 0, 0, 0),
             ),
         ]
         + smalls,

time: 47.7 us -> 45.5 us (0.954)
  Pallas kernels: 46.8 us -> 44.6 us
    pallas_call x1, Pallas kernels: 7.74 us -> 5.61 us  [body(): pl.pallas_call(weight_kernel, grid=(width // step,), out_shape=(jax.Shape...]
where the time goes in v4:
time: 45.5 us; the launch traced here: 45.3 us
  Pallas kernels  44.6 us (98%)
  between operations  0.64 us (1%)
    pallas_call x1, Pallas kernels, body(): pl.pallas_call(functools.partial(kernel, n_fsdp, n_ep, chunks), out_shape...  39 us
    pallas_call x1, Pallas kernels, body(): pl.pallas_call(weight_kernel, grid=(width // step,), out_shape=(jax.Shape...  5.61 us

profile of v4, /device:TPU:0, one launch (start us, length us, event | category | flops | bytes accessed | tf_op | source)
XLA Modules:
  0.0 45.3 jit_solution(3300402436075984129)
XLA Ops:
  0.6 39.0 %shard_map.118 = (bf16[8,2048]{1,0:T(8,128)(2,1)}, f32[2,8]{1,0:T(2,128)}, f32[8,8]{1,0:T(8,128)}, bf16[96,512]{1,0:T(8,128)(2,1)}, bf16[96,512]{1,0:T(8,128)(2,1)}, /*index=5*/bf16[2,4,3,96,256]{4,3,2,1,0:T(8,128)(2,1)}) custom-call(bf16[8,2048]{1,0:T(8,128)(2,1)} %tok_ref.1, bf16[8,2048]{1,0:T(8,128)(2,1)} %cot_ref.1, s32[2,8]{1,0:T(2,128)} %bitcast.2, ...), custom_call_target="tpu_custom_call" | custom-call | tf_op jit(solution)/shard_map/pallas_call | solution.py:355
  39.7 5.6 %shard_map.119 = (bf16[8,2048]{1,0:T(8,128)(2,1)}, f32[2,8]{1,0:T(2,128)}, f32[8,8]{1,0:T(8,128)}, bf16[512,2048]{1,0:T(8,128)(2,1)}, bf16[512,2048]{1,0:T(8,128)(2,1)}, /*index=5*/bf16[2048,512]{1,0:T(8,128)(2,1)}) custom-call(bf16[96,512]{1,0:T(8,128)(2,1)} %get-tuple-element.18.x_ref, bf16[96,512]{1,0:T(8,128)(2,1)} %get-tuple-element.19.dy_ref, ...), custom_call_target="tpu_custom_call" | custom-call | tf_op jit(solution)/shard_map/pallas_call | solution.py:416
